TPU v7x, 32 devices: a whole 2x2x4 slice. The times are simulated.
32 devices in a mesh: rows: 8 (over z, x), cols: 4 (over y, core).
Axes of the slice: x: 2, y: 2, z: 4, core: 2. Of those that a mesh axis runs over, the one named last changes fastest.
Arguments:
- basis: bfloat16 [65536, 512], P('rows', 'cols'), may hold values from -6 to 6
- lower: bfloat16 [256, 256, 256], P('rows'), may hold values from -0.375 to 0.375
- diag: bfloat16 [256, 256, 256], P('rows'), may hold values from -0.375 to 0.375
- upper: bfloat16 [256, 256, 256], P('rows'), may hold values from -0.375 to 0.375
- inverse: bfloat16 [256, 256, 256], P('rows'), may hold values from -0.375 to 0.375
Outputs:
- ortho: bfloat16 [65536, 512], P('rows', 'cols')
- projected: float32 [512, 512], P(None, 'cols')
All inputs are finite; a program needn't handle non-finite values.
Results may differ from a plain program's by a relative error of at most 0.0085.
Values may be sent and summed in bfloat16 or wider, within the bound.
A program may use at most 128 MiB of HBM per device.

v0:
```python
import functools

import jax
import jax.numpy as jnp
from jax import lax
from jax.experimental import pallas as pl
from jax.experimental.pallas import tpu as pltpu
from jax.sharding import PartitionSpec as P

LANES = 128
MESH = pl.DeviceIdType.MESH
VMEM = pl.BlockSpec(memory_space=pltpu.VMEM)
ANY = pl.BlockSpec(memory_space=pl.ANY)
SUB = 8
HI = lax.Precision.HIGHEST

def factor_tile(block, hold):
    size = block.shape[0]
    wide = (SUB, size)
    tiles = size // SUB
    row_of = lax.broadcasted_iota(jnp.int32, wide, 0)
    lane_of = lax.broadcasted_iota(jnp.int32, wide, 1)
    a = [block[t * SUB:(t + 1) * SUB, :] for t in range(tiles)]
    out = []
    for t in range(tiles):
        base = t * SUB
        at = a[t]
        last = t == tiles - 1
        inside = (lane_of >= base) & (lane_of < base + SUB)
        unity = jnp.where(lane_of == row_of + base, 1.0, 0.0).astype(jnp.float32)
        mixed = jnp.where(inside, unity, at)
        pivot = {}
        for j in range(SUB):
            hold[t % 2, j] = jnp.broadcast_to(at[:, base + j:base + j + 1], wide)
        for j in range(SUB):
            for i in range(j, SUB):
                pivot[i, j] = hold[t % 2, j, pl.ds(i, SUB, stride=0), :]
        rows = [jnp.broadcast_to(mixed[i:i + 1, :], wide) for i in range(SUB)]
        unit = {}
        solved = [None] * SUB
        if not last:
            ahead = jnp.where(inside, 0.0, a[t + 1])
            edge = [jnp.broadcast_to(a[t + 1][:, base + j:base + j + 1], wide) for j in range(SUB)]
        fin = jnp.zeros(wide, jnp.float32)
        for j in range(SUB):
            d = pivot[j, j]
            root = lax.rsqrt(d)
            inv = 1.0 / d
            for i in range(j + 1, SUB):
                unit[i, j] = pivot[i, j] * inv
            for i in range(j + 1, SUB):
                for q in range(j + 1, i + 1):
                    pivot[i, q] = pivot[i, q] - unit[i, j] * pivot[q, j]
            for i in range(j + 1, SUB):
                rows[i] = rows[i] - unit[i, j] * rows[j]
            fin = jnp.where(row_of == j, rows[j] * root, fin)
            if not last:
                solved[j] = rows[j] * inv
                ahead = ahead - edge[j] * solved[j]
                for q in range(j + 1, SUB):
                    edge[q] = edge[q] - edge[j] * unit[q, j]
        out.append(jnp.where(lane_of < base + SUB, fin, 0.0))
        if last:
            break
        a[t + 1] = ahead
        if t + 2 < tiles:
            for j in range(SUB - 1, -1, -1):
                for i in range(j):
                    solved[i] = solved[i] - unit[j, i] * solved[j]
        for s in range(t + 2, tiles):
            new = jnp.where(inside, 0.0, a[s])
            for j in range(SUB - 1, -1, -1):
                c = jnp.broadcast_to(a[s][:, base + j:base + j + 1], wide)
                new = new - c * solved[j]
            a[s] = new
    return jnp.concatenate(out, axis=0)


def eliminate(work_ref, b, out_ref, panel_ref, hold_ref):
    n, size, _ = work_ref.shape
    at = [work_ref[b, :, i * size:(i + 1) * size] for i in range(n)]
    block = at[0]
    for i in range(1, n):
        block = jnp.where(b == i, at[i], block)
    panel_ref[...] = factor_tile(block, hold_ref)

    def stage(k):
        linv = panel_ref[...]
        rows = slice(k * size, (k + 1) * size)
        if k:
            out_ref[rows, :k * size] = fine(linv, out_ref[rows, :k * size])
        out_ref[rows, rows] = linv
        if k + 1 < n:
            out_ref[rows, (k + 1) * size:] = jnp.zeros((size, (n - k - 1) * size), jnp.float32)
            right = fine(linv, work_ref[k, :, (k + 1) * size:n * size])
            known = jnp.concatenate([right, out_ref[rows, :(k + 1) * size]], axis=1)
            for i in range(k + 1, n):
                step = fine(right[:, (i - k - 1) * size:(i - k) * size], known, ((0,), (0,)))
                lines = slice(i * size, (i + 1) * size)
                cut = (n - k - 1) * size
                work_ref[i, :, (k + 1) * size:n * size] = work_ref[i, :, (k + 1) * size:n * size] - step[:, :cut]
                if k:
                    out_ref[lines, :k * size] = out_ref[lines, :k * size] - step[:, cut:cut + k * size]
                out_ref[lines, rows] = -step[:, cut + k * size:]

    for k in range(n):
        pl.when(b == k)(functools.partial(stage, k))


def dot(left, right):
    return jnp.dot(left, right, preferred_element_type=jnp.float32)


def inner(left, right):
    return lax.dot_general(
        left, right, (((0,), (0,)), ((), ())), preferred_element_type=jnp.float32
    )


def fine(left, right, dims=((1,), (0,))):
    return lax.dot_general(
        left, right, (dims, ((), ())), precision=HI, preferred_element_type=jnp.float32
    )


def remote(src, dst, send, recv, **where):
    return pltpu.make_async_remote_copy(
        src_ref=src, dst_ref=dst, send_sem=send, recv_sem=recv, device_id=where, device_id_type=MESH
    )


def exchange(count, me, where, source, target, whole, send, recv):
    for step in range(1, count):
        peer = lax.rem(me + step, count)
        remote(source(peer), target(me), send, recv, **where(peer)).start()

    def finish():
        if count > 1:
            remote(whole, whole, send, recv, **where(lax.rem(me + 1, count))).wait()

    return finish


def around(nr, nc, r, c):
    h = nc // 2
    for step in range(1, nc):
        yield True, r, lax.rem(c + step, nc)
    for by in (1, -1):
        there = (r + by >= 0) & (r + by < nr)
        for k in range(h):
            yield there, r + by, (c // h) * h + k
    for by in (2, -2):
        yield (r + by >= 0) & (r + by < nr), r + by, c


def rounds(nr, nc):
    h = nc // 2
    seen, edge, far = {(0, 0)}, {(0, 0)}, 0
    while len(seen) < nr * nc:
        new = set()
        for r, c in edge:
            new |= {(r, k) for k in range(nc)}
            new |= {(r + by, c // h * h + k) for by in (1, -1) for k in range(h)}
            new |= {(r + by, c) for by in (2, -2)}
        edge = {d for d in new if 0 <= d[0] < nr} - seen
        seen |= edge
        far += 1
    return far


def tell(sem, nr, nc, r, c):
    for there, row, col in around(nr, nc, r, c):
        def signal():
            pl.semaphore_signal(sem, inc=1, device_id=dict(rows=row, cols=col), device_id_type=MESH)

        if there is True:
            signal()
        else:
            pl.when(there)(signal)


def hear(sem, nr, nc, r, c):
    pl.semaphore_wait(sem, sum(1 if t is True else t.astype(jnp.int32) for t, _, _ in around(nr, nc, r, c)))


def lined(ref, start, extent):
    return ref.at[pl.ds(pl.multiple_of(start, 8), extent), :]


def summed(ref, count):
    return sum((ref[k] for k in range(1, count)), ref[0])


def whole_kernel(
    nr, nc, basis, lower, diag, upper, inverse, ortho, projected,
    bext, wext, wsend, oext, held, gy, gx, total, rinv, cwork, cpanel, hold, linv0, linv1, tall,
    ypack, ygot1, ypart, ygot2, yall, xpack, xgot1, xpart, xgot2, xall,
    pgot1, phalf, pgot2, psum, ppack, pall,
    far, home, zext, mix,
    known, wsem, bsend, brecv, esem, osem, orecv, hsend, hrecv, fsend, frecv, isem, msend, mrecv, *sems,
):
    sems = list(sems)

    def pair():
        return sems.pop(0), sems.pop(0)

    bf16, f32 = jnp.bfloat16, jnp.float32
    r, c = lax.axis_index("rows"), lax.axis_index("cols")
    h = nc // 2
    y, p = c // h, lax.rem(c, h)
    other = (1 - y) * h + p
    _, _, count, size, _ = held.shape
    width = basis.shape[1]
    half = width * h
    order = 2 * half
    body = count * size
    bottom = size + body
    team = 2 * nr
    seat = 2 * r + y

    def mate(k):
        return dict(cols=y * h + k)

    def member(k):
        return dict(rows=k // 2, cols=lax.rem(k, 2) * h + p)

    def line(k):
        return dict(rows=k)

    def at(i):
        return pl.ds(pl.multiple_of(i * size, size), size)

    def lanes(k, extent):
        return pl.ds(pl.multiple_of(k * extent, LANES), extent)

    wl, wd, wu, wi = (held.at[:, k] for k in range(4))
    for j, g in enumerate((other, c)):
        for k, part in enumerate((lower, diag, upper, inverse)):
            pltpu.make_async_copy(part.at[pl.ds(g * count, count)], held.at[j, k], wsem.at[j]).start()

    def weighed(j):
        pltpu.make_async_copy(held.at[1 - j], held.at[j], wsem.at[j]).wait()

    spans = [(0, size), (size, body), (bottom, size)]

    def group(j, k):
        return y * h + k if j else (1 - y) * h + k

    def leaving(j, s, k):
        start, extent = spans[s]
        return basis.at[pl.ds(pl.multiple_of(group(j, k) * body - size + start, size), extent), :]

    def landing(j, s, k):
        start, extent = spans[s]
        return bext.at[j, pl.ds(start, extent), lanes(k, width)]

    def within(s, g, action):
        if s == 0:
            pl.when(g > 0)(action)
        elif s == 2:
            pl.when(g < nc - 1)(action)
        else:
            action()

    def own(j, s):
        return pltpu.make_async_copy(leaving(j, s, p), landing(j, s, p), brecv.at[j, s])

    def to_mate(j, s, step):
        k = lax.rem(p + step, h)
        return remote(leaving(j, s, k), landing(j, s, p), bsend.at[j, s], brecv.at[j, s], **mate(k))

    def down():
        return remote(
            basis.at[pl.ds(nc * body - size, size), :], landing(1 - y, 0, p), esem.at[0],
            brecv.at[1 - y, 0], rows=r + 1, cols=y * h,
        )

    def up():
        return remote(
            basis.at[pl.ds(0, size), :], landing(y, 2, p), esem.at[1],
            brecv.at[y, 2], rows=r - 1, cols=y * h + h - 1,
        )

    for j in (0, 1):
        for s in (1, 0, 2):
            within(s, group(j, p), lambda: own(j, s).start())

    barrier = pltpu.get_barrier_semaphore()
    tell(barrier, nr, nc, r, c)
    hear(barrier, nr, nc, r, c)
    heard = known.shape[0]
    tell(known.at[0], nr, nc, r, c)
    told = [0]

    def spread():
        if told[0] < heard:
            hear(known.at[told[0]], nr, nc, r, c)
            told[0] += 1
            if told[0] < heard:
                tell(known.at[told[0]], nr, nc, r, c)

    def each(j, s, action):
        for step in range(1, h):
            k = lax.rem(p + step, h)
            within(s, group(j, k), functools.partial(action, step))

    for step in range(1, h):
        to_mate(0, 1, step).start()
    pl.when(r < nr - 1)(lambda: down().start())
    pl.when(r > 0)(lambda: up().start())
    for j, s in ((0, 0), (0, 2), (1, 1), (1, 0), (1, 2)):
        each(j, s, lambda step: to_mate(j, s, step).start())

    for j in (0, 1):
        @pl.when((r == 0) & (group(j, p) == 0))
        def _():
            bext[j, 0:size, :] = jnp.zeros((size, half), bf16)

        @pl.when((r == nr - 1) & (group(j, p) == nc - 1))
        def _():
            bext[j, bottom:bottom + size, :] = jnp.zeros((size, half), bf16)

    @pl.when((r == 0) & (c == 0))
    def _():
        wext[0:size, :] = jnp.zeros((size, order), bf16)

    @pl.when((r == nr - 1) & (c == nc - 1))
    def _():
        wext[bottom:bottom + size, :] = jnp.zeros((size, order), bf16)

    def arrive(j, s):
        g = group(j, p)
        start, extent = spans[s]
        full = bext.at[j, pl.ds(start, extent), :]
        comes = {0: (g > 0) | (r > 0), 1: r >= 0, 2: (g < nc - 1) | (r < nr - 1)}[s]
        pl.when(comes)(lambda: pltpu.make_async_copy(bext.at[1 - j, pl.ds(start, extent), :], full, brecv.at[j, s]).wait())

    def applied(field, j, some, columns, out):
        for i in some:
            mixed = (
                dot(wl[j, i], field[i * size:(i + 1) * size, columns])
                + dot(wd[j, i], field[(i + 1) * size:(i + 2) * size, columns])
                + dot(wu[j, i], field[(i + 2) * size:(i + 3) * size, columns])
            )
            mix[j, i * size:(i + 1) * size, :] = mixed.astype(bf16)
        for i in some:
            out(i, dot(wi[j, i], mix[j, i * size:(i + 1) * size, :]).astype(bf16))

    mine = lanes(y, half)
    chunks = [(1, 1), (2, 1)] + [(i, 2) for i in range(3, count - 1, 2)] + [(0, 1), (count - 1, 1)]

    def cross(n, to=None):
        start, extent = chunks[n][0] * size, chunks[n][1] * size
        return remote(
            wsend.at[pl.ds(start, extent), :],
            wext.at[pl.ds(size + start, extent), mine if to is None else to],
            osem, orecv, cols=other,
        )

    weighed(0)
    arrive(0, 1)

    def first(some):
        def keep(i, w):
            wsend[i * size:(i + 1) * size, :] = w

        applied(bext.at[0], 0, some, slice(None), keep)

    def second(some):
        def keep(i, w):
            wext[(i + 1) * size:(i + 2) * size, mine] = w

        applied(bext.at[1], 1, some, slice(None), keep)

    for n in range(len(chunks) - 2):
        start, extent = chunks[n]
        first(range(start, start + extent))
        cross(n).start()
        if n == 1:
            spread()
    weighed(1)
    arrive(1, 1)
    second(range(1, count - 1))
    spread()
    mid = slice(size, body - size)
    gy[...] = inner(wsend[mid, :], wsend[mid, :])
    spread()
    own_half = wext[2 * size:body, mine]
    gy[...] += inner(own_half, own_half)
    arrive(0, 0)
    arrive(0, 2)
    first((0, count - 1))
    for n in range(len(chunks) - 2, len(chunks)):
        cross(n).start()
    spread()
    arrive(1, 0)
    arrive(1, 2)
    second((0, count - 1))
    for _ in range(heard):
        spread()
    for rows in (slice(0, size), slice(body - size, body)):
        own_half = wext[rows.start + size:rows.stop + size, mine]
        gy[...] += inner(wsend[rows, :], wsend[rows, :]) + inner(own_half, own_half)

    early = list(range(len(chunks) // 2))
    late = sorted(range(len(chunks) // 2, len(chunks)), key=lambda n: chunks[n][1])

    def further(n):
        start, extent = chunks[n][0] * size, chunks[n][1] * size
        if n in early:
            source, target = wext.at[pl.ds(size + start, extent), :half], far.at[pl.ds(start, extent), :]
        else:
            source, target = oext.at[1, pl.ds(size + start, extent), :], home.at[pl.ds(start, extent), :]
        return remote(source, target, fsend.at[int(n in late)], frecv.at[int(n in late)], cols=other)

    def all_further(kind):
        some = (early, late)[kind]
        extent = sum(chunks[n][1] for n in some) * size
        part = far.at[pl.ds(0, extent), :]
        return remote(part, part, fsend.at[kind], frecv.at[kind], cols=other)

    def send_late(some):
        for n in some:
            further(n).start()

    across = half // LANES
    place = 0
    for i in range(across):
        for j in range(i, across):
            ypack[place * LANES:(place + 1) * LANES, :] = gy[
                i * LANES:(i + 1) * LANES, j * LANES:(j + 1) * LANES
            ]
            place += 1
    if ypack.shape[0] > place * LANES:
        ypack[place * LANES:, :] = jnp.zeros((ypack.shape[0] - place * LANES, LANES), f32)
    share, piece = ygot1.shape[1], ygot2.shape[1]
    s, v = pair()
    finish = exchange(
        h, p, mate, lambda d: lined(ypack, d * share, share), lambda k: ygot1.at[k],
        ygot1.at[pl.ds(0, h - 1)], s, v
    )
    ygot1[p] = ypack[pl.ds(pl.multiple_of(p * share, 8), share), :]
    finish()
    ypart[...] = summed(ygot1, h)
    s, v = pair()
    finish = exchange(
        nr, r, line, lambda d: lined(ypart, d * piece, piece), lambda k: ygot2.at[k],
        ygot2.at[pl.ds(0, nr - 1)], s, v
    )
    ygot2[r] = ypart[pl.ds(pl.multiple_of(r * piece, 8), piece), :]
    finish()

    def yspot(k):
        return yall.at[y, pl.ds(pl.multiple_of(p * share + k * piece, 8), piece), :]

    def yshare(side, k):
        return yall.at[side, pl.ds(pl.multiple_of(k * share, 8), share), :]

    yall[y, pl.ds(pl.multiple_of(p * share + r * piece, 8), piece), :] = summed(ygot2, nr)
    s, v = pair()
    exchange(nr, r, line, lambda d: yspot(r), lambda k: yspot(r), ygot2.at[pl.ds(0, nr - 1)], s, v)()
    s, v = pair()
    over = remote(yshare(y, p), yshare(y, p), s, v, cols=other)
    over.start()

    def both(side, sems_of):
        rest = yall.at[side, pl.ds(0, (h - 1) * share), :]
        exchange(h, p, mate, lambda d: yshare(side, p), lambda k: yshare(side, p), rest, *sems_of)()

    both(y, pair())
    opposite_sems = pair()

    def opposite():
        over.wait_recv()
        both(1 - y, opposite_sems)

    def load(which):
        place = 0
        for i in range(across):
            for j in range(i, across):
                cwork[i, :, j * LANES:(j + 1) * LANES] = yall[which, place * LANES:(place + 1) * LANES, :]
                place += 1

    flat = r * nc + c
    last = nr * nc - 1

    def halo(kind, q):
        start = (body, size)[kind]
        target = (0, bottom)[kind]
        to = flat + (1, -1)[kind]
        part = pl.ds(q * half, half)
        return remote(
            wext.at[pl.ds(start, size), part], wext.at[pl.ds(target, size), part], hsend.at[kind, q],
            hrecv.at[kind, q], rows=to // nc, cols=lax.rem(to, nc),
        )


    theirs = lanes(1 - y, half)
    xshare, xpiece = xgot1.shape[1], xgot2.shape[1]
    def xspot(k):
        return lined(xall, p * xshare + k * xpiece, xpiece)
    def xsection(k):
        return lined(xall, k * xshare, xshare)
    xcore, xscatter, xgather, xcopy = pair(), pair(), pair(), pair()

    def scatter():
        return exchange(
            team, seat, member, lambda d: lined(xpart, d * xpiece, xpiece), lambda k: xgot2.at[k],
            xgot2.at[pl.ds(0, team - 1)], *xscatter,
        )

    def turned(columns):
        depth = columns.stop
        oext[columns.start // half, size:bottom, :] = dot(wext[size:bottom, :depth], rinv[:depth, columns]).astype(bf16)

    def imaged(q):
        def keep(i, z):
            zext[q, i * size:(i + 1) * size, :] = z

        applied(oext.at[q], 1, range(count), slice(None), keep)

    def cross_half():
        crossed = wext.at[pl.ds(size, body), theirs]
        remote(crossed, crossed, osem, orecv, cols=other).wait_recv()
        gx[...] = inner(wext[size:bottom, :half], wext[size:bottom, half:])
        for j in range(across):
            xpack[j * half:(j + 1) * half, :] = gx[:, j * LANES:(j + 1) * LANES]
        if xpack.shape[0] > across * half:
            xpack[across * half:, :] = jnp.zeros((xpack.shape[0] - across * half, LANES), f32)
        finish = exchange(
            h, p, mate, lambda d: lined(xpack, d * xshare, xshare), lambda k: xgot1.at[k],
            xgot1.at[pl.ds(0, h - 1)], *xcore
        )
        xgot1[p] = xpack[pl.ds(pl.multiple_of(p * xshare, 8), xshare), :]
        finish()
        xpart[...] = summed(xgot1, h)
        scatter()
        pl.when(flat < last)(lambda: halo(0, 0).start())
        pl.when(flat > 0)(lambda: halo(1, 0).start())

    def join():
        pl.when(y == 0)(opposite)
        arrived = xgot2.at[pl.ds(0, team - 1)]
        remote(arrived, arrived, *xscatter, **member(lax.rem(seat + 1, team))).wait()
        xgot2[seat] = xpart[pl.ds(pl.multiple_of(seat * xpiece, 8), xpiece), :]
        xall[pl.ds(pl.multiple_of(p * xshare + seat * xpiece, 8), xpiece), :] = summed(xgot2, team)
        exchange(team, seat, member, lambda d: xspot(seat), lambda k: xspot(seat), arrived, *xgather)
        pl.when(flat < last)(lambda: halo(0, 1).start())
        pl.when(flat > 0)(lambda: halo(1, 1).start())

        @pl.when(y == 0)
        def _():
            for n in early:
                further(n).start()

    def rest():
        linv0[...] = linv1[...]
        rinv[:half, :half] = linv0[...].T.astype(bf16)
        turned(slice(0, half))

        def early_image():
            pl.when(flat > 0)(lambda: halo(0, 0).wait_recv())
            pl.when(flat < last)(lambda: halo(1, 0).wait_recv())
            oext[0, :size, :] = dot(wext[:size, :half], rinv[:half, :half]).astype(bf16)
            oext[0, bottom:, :] = dot(wext[bottom:, :half], rinv[:half, :half]).astype(bf16)
            imaged(0)
            total[:half, :half] = inner(oext[0, size:bottom, :], zext[0])

        pl.when(y == 0)(early_image)
        arrived = xgot2.at[pl.ds(0, team - 1)]
        remote(arrived, arrived, *xgather, **member(lax.rem(seat + 1, team))).wait()
        finish = exchange(
            h, p, mate, lambda d: xsection(p), lambda k: xsection(p), lined(xall, 0, (h - 1) * xshare), *xcopy
        )
        pl.when(y == 1)(early_image)
        finish()
        for j in range(across):
            gx[:, j * LANES:(j + 1) * LANES] = xall[j * half:(j + 1) * half, :]
        tall[...] = fine(linv0[...], gx[...])
        load(1)
        for i in range(across):
            cwork[i, :, i * LANES:] = cwork[i, :, i * LANES:] - fine(
                tall[:, i * LANES:(i + 1) * LANES], tall[:, i * LANES:], ((0,), (0,))
            )
        gx[...] = fine(tall[...], linv0[...], ((0,), (0,)))

    pl.when(y == 0)(lambda: load(0))

    def factor_step(g, carry):
        @pl.when((g == 0) & (y == 1))
        def _():
            cross_half()
            opposite()
            load(0)

        eliminate(cwork, lax.rem(g, across), linv1, cpanel, hold)
        pl.when((g == 0) & (y == 0))(cross_half)
        pl.when(((g == 0) & (y == 1)) | ((g == across - 1) & (y == 0)))(join)
        pl.when(g == across - 1)(rest)
        return carry

    lax.fori_loop(0, 2 * across, factor_step, 0)
    rinv[half:, half:] = linv1[...].T.astype(bf16)
    rinv[:half, half:] = (-fine(gx[...], linv1[...], ((0,), (1,)))).astype(bf16)
    pl.when(flat > 0)(lambda: halo(0, 1).wait_recv())
    pl.when(flat < last)(lambda: halo(1, 1).wait_recv())
    oext[1] = dot(wext[...], rinv[:, half:]).astype(bf16)
    pl.when(y == 0)(lambda: send_late(late[:1]))
    imaged(1)
    total[:half, half:] = inner(oext[0, size:bottom, :], zext[1])
    def place(j, source, first, k):
        return source.at[pl.ds(first, body), k], ortho.at[pl.ds(pl.multiple_of((c if j else other) * body, size), body), :]

    def settle(j):
        source, first = (oext.at[y], size) if j else (home, 0)

        def col(k):
            return lanes(k, width)

        own_copy = pltpu.make_async_copy(*place(j, source, first, col(p)), isem.at[j])
        own_copy.start()
        for step in range(1, h):
            k = lax.rem(p + step, h)
            src_ref, dst_ref = place(j, source, first, col(k))
            remote(src_ref, dst_ref, msend.at[j], mrecv.at[j], **mate(k)).start()

        def finish():
            own_copy.wait()
            if h > 1:
                moved = ortho.at[pl.ds(0, (h - 1) * body), :]
                remote(moved, moved, msend.at[j], mrecv.at[j], **mate(lax.rem(p + 1, h))).wait()

        return finish

    parts = psum.shape[0]
    rows_of = order // parts
    lump = rows_of // nr
    sends = [pair() for _ in range(4)]

    def band(n):
        return slice(n * rows_of, (n + 1) * rows_of)

    def share_of(n):
        for k in range(2):
            for q in range(h):
                ppack[n, q, k] = total[band(n), (k * h + q) * width:(k * h + q + 1) * width].astype(bf16)
        s, v = sends[0]
        return exchange(
            h, p, mate, lambda d: ppack.at[n, d], lambda k: pgot1.at[n, k], pgot1.at[n, pl.ds(0, h - 1)], s.at[n], v.at[n]
        )

    def crossing(n):
        s, v = sends[1]
        return remote(phalf.at[n, 0], phalf.at[n, 1], s.at[n], v.at[n], cols=other)

    def joined(n, k):
        mine_here = total[band(n), lanes(k * h + p, width)]
        for step in range(1, h):
            mine_here = mine_here + pgot1[n, lax.rem(p + step, h), k].astype(f32)
        return mine_here

    def launch(n):
        phalf[n, 0] = joined(n, 1 - y).astype(bf16)
        crossing(n).start()

    def spot(n, k):
        return psum.at[n, pl.ds(pl.multiple_of(k * lump, lump), lump), :]

    def scattered(n):
        crossing(n).wait()
        psum[n] = (joined(n, y) + phalf[n, 1].astype(f32)).astype(bf16)
        s, v = sends[2]
        done = exchange(
            nr, r, line, lambda d: spot(n, d), lambda k: pgot2.at[n, k], pgot2.at[n, pl.ds(0, nr - 1)], s.at[n], v.at[n]
        )
        pgot2[n, r] = psum[n, pl.ds(pl.multiple_of(r * lump, lump), lump), :]
        return done

    def gathered(n):
        def place_of(k):
            return pall.at[n, pl.ds(pl.multiple_of(k * lump, lump), lump), :]

        pall[n, pl.ds(pl.multiple_of(r * lump, lump), lump), :] = sum(
            (pgot2[n, k].astype(f32) for k in range(1, nr)), pgot2[n, 0].astype(f32)
        ).astype(bf16)
        s, v = sends[3]
        return exchange(nr, r, line, lambda d: place_of(r), lambda k: place_of(r), pgot2.at[n, pl.ds(0, nr - 1)], s.at[n], v.at[n])

    shared = [share_of(n) for n in range(parts // 2)]
    total[half:, :half] = inner(oext[1, size:bottom, :], zext[0])
    total[half:, half:] = inner(oext[1, size:bottom, :], zext[1])
    for n in range(parts // 2):
        shared[n]()
        launch(n)
    shared = [share_of(n) for n in range(parts // 2, parts)]
    for n in range(parts // 2, parts):
        shared[n - parts // 2]()
        launch(n)
    pl.when(y == 0)(lambda: send_late(late[1:]))
    finish_own = settle(1)

    @pl.when(y == 0)
    def _():
        for i in range(count):
            rows = slice(i * size, (i + 1) * size)
            home[rows, :] = dot(wsend[rows, :], rinv[:half, :half]).astype(bf16)

    spread_out = [scattered(n) for n in range(parts)]

    @pl.when(y == 1)
    def _():
        all_further(0).wait_recv()
        for i in (i for n in early for i in range(chunks[n][0], sum(chunks[n]))):
            rows = slice(i * size, (i + 1) * size)
            home[rows, :] = (dot(far[rows, :], rinv[:half, half:]) + dot(wsend[rows, :], rinv[half:, half:])).astype(bf16)

    brought = []
    for n in range(parts):
        spread_out[n]()
        brought.append(gathered(n))

    @pl.when(y == 1)
    def _():
        all_further(1).wait_recv()

    finish_other = settle(0)
    for n in range(parts):
        brought[n]()
        projected[band(n), :] = pall[n].astype(f32)

    finish_own()
    finish_other()

    @pl.when(y == 0)
    def _():
        all_further(0).wait_send()
        all_further(1).wait_send()

    for q in range(2):
        pl.when(flat < last)(lambda: halo(0, q).wait_send())
        pl.when(flat > 0)(lambda: halo(1, q).wait_send())
    remote(wsend, wsend, osem, orecv, cols=other).wait_send()
    over.wait_send()
    pl.when(r < nr - 1)(lambda: down().wait_send())
    pl.when(r > 0)(lambda: up().wait_send())
    for j in (0, 1):
        for s in range(3):
            each(j, s, lambda step: to_mate(j, s, step).wait_send())


def shards(nr, nc, basis, lower, diag, upper, inverse):
    blocks, size, _ = diag.shape
    width = basis.shape[1]
    h = nc // 2
    half = width * h
    order = 2 * half
    count = blocks // nc
    across = half // LANES
    body = count * size
    f32, bf16 = jnp.float32, jnp.bfloat16

    def parcel(lines, parts):
        piece = -(-lines // (h * parts * 8)) * 8
        return piece * parts, piece

    share, piece = parcel(across * (across + 1) // 2 * LANES, nr)
    xshare, xpiece = parcel(across * half, 2 * nr)
    parts = 4 if order // nr >= 8 * SUB else 1
    rows_of = order // parts
    dma = pltpu.SemaphoreType.DMA
    bext = (2, (count + 2) * size, half)
    ext = ((count + 2) * size, order)
    chunks = (count - 4) // 2 + 4
    square = pltpu.VMEM((half, half), f32)
    opflops = 16 * count * size * size * order + 6 * count * size * order * order
    return pl.pallas_call(
        functools.partial(whole_kernel, nr, nc),
        out_shape=(pltpu.VMEM(basis.shape, bf16), pltpu.VMEM((order, width), f32)),
        in_specs=[ANY] * 5,
        out_specs=(VMEM, VMEM),
        scratch_shapes=[
            pltpu.VMEM(bext, bf16), pltpu.VMEM(ext, bf16), pltpu.VMEM((body, half), bf16), pltpu.VMEM(bext, bf16),
            pltpu.VMEM((2, 4, count, size, size), bf16),
            square, square, pltpu.VMEM((order, order), f32), pltpu.VMEM((order, order), bf16),
            pltpu.VMEM((across, LANES, half), f32), pltpu.VMEM((LANES, LANES), f32), pltpu.VMEM((2, SUB, SUB, LANES), f32),
            square, square, square,
            pltpu.VMEM((h * share, LANES), f32), pltpu.VMEM((h, share, LANES), f32), pltpu.VMEM((share, LANES), f32),
            pltpu.VMEM((nr, piece, LANES), f32), pltpu.VMEM((2, h * share, LANES), f32),
            pltpu.VMEM((h * xshare, LANES), f32), pltpu.VMEM((h, xshare, LANES), f32), pltpu.VMEM((xshare, LANES), f32),
            pltpu.VMEM((2 * nr, xpiece, LANES), f32), pltpu.VMEM((h * xshare, LANES), f32),
            pltpu.VMEM((parts, h, 2, rows_of, width), bf16), pltpu.VMEM((parts, 2, rows_of, width), bf16),
            pltpu.VMEM((parts, nr, rows_of // nr, width), bf16), pltpu.VMEM((parts, rows_of, width), bf16),
            pltpu.VMEM((parts, h, 2, rows_of, width), bf16), pltpu.VMEM((parts, rows_of, width), bf16),
            pltpu.VMEM((body, half), bf16), pltpu.VMEM((body, half), bf16), pltpu.VMEM((2, body, half), bf16),
            pltpu.VMEM((2, body, half), bf16),
            pltpu.SemaphoreType.REGULAR((rounds(nr, nc) - 1,)),
            dma((2,)), dma((2, 3)), dma((2, 3)), dma((2,)),
            dma, dma, dma((2, 2)), dma((2, 2)), dma((2,)), dma((2,)),
            dma((2,)), dma((2,)), dma((2,)),
        ] + [dma] * 20 + [dma((parts,))] * 8,
        compiler_params=pltpu.CompilerParams(has_side_effects=True, collective_id=1),
        cost_estimate=pl.CostEstimate(flops=opflops, bytes_accessed=1 << 24, transcendentals=0),
        name="krylov",
    )(basis, lower, diag, upper, inverse)


def solution(mesh):
    in_specs = (
        P("rows", "cols"),
        P("rows", None, None),
        P("rows", None, None),
        P("rows", None, None),
        P("rows", None, None),
    )
    out_specs = (P("rows", "cols"), P(None, "cols"))
    body = functools.partial(shards, mesh.shape["rows"], mesh.shape["cols"])
    return jax.shard_map(body, mesh=mesh, in_specs=in_specs, out_specs=out_specs, check_vma=False)
```

profile of v0, /device:TPU:0, one launch (start us, length us, event | category | flops | bytes accessed | tf_op | source)
XLA Modules:
  0.0 76.3 jit_solution(7297212908327768929)
XLA Ops:
  0.6 73.7 %krylov.1 = (bf16[8192,128]{1,0:T(8,128)(2,1)S(1)}, f32[512,128]{1,0:T(8,128)S(1)}) custom-call(bf16[8192,128]{1,0:T(8,128)(2,1)} %basis.1, bf16[32,256,256]{2,1,0:T(8,128)(2,1)} %lower.1, bf16[32,256,256]{2,1,0:T(8,128)(2,1)} %diag.1, bf16[32,256,256]{2,1,0:T(8,128)(2,1)} %upper.1, bf16[32,256,256]{2,1,0:T(8,128)(2,1)} %inverse.1), custom_call_target="tpu_custom_call" | custom-call | flops 7516192768 | bytes 16777216 | tf_op jit(solution)/shard_map/krylov/pallas_call | solution.py:776
  74.3 1.3 %copy.9 = bf16[8192,128]{1,0:T(8,128)(2,1)} copy(bf16[8192,128]{1,0:T(8,128)(2,1)S(1)} %get-tuple-element.2) | data formatting | bytes 4194304
  75.6 0.7 copy.10
where the time goes:
time: 76.5 us; the launch traced here: 76.3 us
  Pallas kernels  73.7 us (96%)
  local copies, waits for them, and re-layouts  2.02 us (3%)
    pallas_call x1, Pallas kernels, shards(): pl.pallas_call(functools.partial(whole_kernel, nr, nc), out_shape=(pltpu....  73.7 us
    unnamed x2, local copies, waits for them, and re-layouts  2.02 us

commit v1 on v0

--- a/solution.py
+++ b/solution.py
@@ -241,7 +241,7 @@
     def weighed(j):
         pltpu.make_async_copy(held.at[1 - j], held.at[j], wsem.at[j]).wait()
 
-    spans = [(0, size), (size, body), (bottom, size)]
+    spans = [(0, size), (size, 3 * size), (bottom, size), (4 * size, body - 3 * size)]
 
     def group(j, k):
         return y * h + k if j else (1 - y) * h + k
@@ -282,7 +282,7 @@
         )
 
     for j in (0, 1):
-        for s in (1, 0, 2):
+        for s in (1, 3, 0, 2):
             within(s, group(j, p), lambda: own(j, s).start())
 
     barrier = pltpu.get_barrier_semaphore()
@@ -304,11 +304,12 @@
             k = lax.rem(p + step, h)
             within(s, group(j, k), functools.partial(action, step))
 
-    for step in range(1, h):
-        to_mate(0, 1, step).start()
+    for s in (1, 3):
+        for step in range(1, h):
+            to_mate(0, s, step).start()
     pl.when(r < nr - 1)(lambda: down().start())
     pl.when(r > 0)(lambda: up().start())
-    for j, s in ((0, 0), (0, 2), (1, 1), (1, 0), (1, 2)):
+    for j, s in ((0, 0), (0, 2), (1, 1), (1, 3), (1, 0), (1, 2)):
         each(j, s, lambda step: to_mate(j, s, step).start())
 
     for j in (0, 1):
@@ -332,7 +333,7 @@
         g = group(j, p)
         start, extent = spans[s]
         full = bext.at[j, pl.ds(start, extent), :]
-        comes = {0: (g > 0) | (r > 0), 1: r >= 0, 2: (g < nc - 1) | (r < nr - 1)}[s]
+        comes = {0: (g > 0) | (r > 0), 2: (g < nc - 1) | (r < nr - 1)}.get(s, r >= 0)
         pl.when(comes)(lambda: pltpu.make_async_copy(bext.at[1 - j, pl.ds(start, extent), :], full, brecv.at[j, s]).wait())
 
     def applied(field, j, some, columns, out):
@@ -374,12 +375,15 @@
 
     for n in range(len(chunks) - 2):
         start, extent = chunks[n]
+        if n == 1:
+            arrive(0, 3)
         first(range(start, start + extent))
         cross(n).start()
         if n == 1:
             spread()
     weighed(1)
     arrive(1, 1)
+    arrive(1, 3)
     second(range(1, count - 1))
     spread()
     mid = slice(size, body - size)
@@ -744,7 +748,7 @@
     pl.when(r < nr - 1)(lambda: down().wait_send())
     pl.when(r > 0)(lambda: up().wait_send())
     for j in (0, 1):
-        for s in range(3):
+        for s in range(4):
             each(j, s, lambda step: to_mate(j, s, step).wait_send())
 
 
@@ -794,7 +798,7 @@
             pltpu.VMEM((body, half), bf16), pltpu.VMEM((body, half), bf16), pltpu.VMEM((2, body, half), bf16),
             pltpu.VMEM((2, body, half), bf16),
             pltpu.SemaphoreType.REGULAR((rounds(nr, nc) - 1,)),
-            dma((2,)), dma((2, 3)), dma((2, 3)), dma((2,)),
+            dma((2,)), dma((2, 4)), dma((2, 4)), dma((2,)),
             dma, dma, dma((2, 2)), dma((2, 2)), dma((2,)), dma((2,)),
             dma((2,)), dma((2,)), dma((2,)),
         ] + [dma] * 20 + [dma((parts,))] * 8,

time: 76.5 us -> 76.2 us (level)
  no operation moved by 1% of the time
where the time goes in v1:
time: 76.2 us; the launch traced here: 76 us
  Pallas kernels  73.4 us (96%)
  local copies, waits for them, and re-layouts  2.02 us (3%)
    pallas_call x1, Pallas kernels, shards(): pl.pallas_call(functools.partial(whole_kernel, nr, nc), out_shape=(pltpu....  73.4 us
    unnamed x2, local copies, waits for them, and re-layouts  2.02 us

profile of v1, /device:TPU:0, one launch (start us, length us, event | category | flops | bytes accessed | tf_op | source)
XLA Modules:
  0.0 76.0 jit_solution(17404315930305633788)
XLA Ops:
  0.6 73.4 %krylov.1 = (bf16[8192,128]{1,0:T(8,128)(2,1)S(1)}, f32[512,128]{1,0:T(8,128)S(1)}) custom-call(bf16[8192,128]{1,0:T(8,128)(2,1)} %basis.1, bf16[32,256,256]{2,1,0:T(8,128)(2,1)} %lower.1, bf16[32,256,256]{2,1,0:T(8,128)(2,1)} %diag.1, bf16[32,256,256]{2,1,0:T(8,128)(2,1)} %upper.1, bf16[32,256,256]{2,1,0:T(8,128)(2,1)} %inverse.1), custom_call_target="tpu_custom_call" | custom-call | flops 7516192768 | bytes 16777216 | tf_op jit(solution)/shard_map/krylov/pallas_call | solution.py:780
  74.0 1.3 %copy.9 = bf16[8192,128]{1,0:T(8,128)(2,1)} copy(bf16[8192,128]{1,0:T(8,128)(2,1)S(1)} %get-tuple-element.2) | data formatting | bytes 4194304
  75.3 0.7 copy.10

commit v2 on v1

--- a/solution.py
+++ b/solution.py
@@ -543,7 +543,6 @@
         pl.when(flat > 0)(lambda: halo(1, 0).start())
 
     def join():
-        pl.when(y == 0)(opposite)
         arrived = xgot2.at[pl.ds(0, team - 1)]
         remote(arrived, arrived, *xscatter, **member(lax.rem(seat + 1, team))).wait()
         xgot2[seat] = xpart[pl.ds(pl.multiple_of(seat * xpiece, 8), xpiece), :]
@@ -571,6 +570,7 @@
             total[:half, :half] = inner(oext[0, size:bottom, :], zext[0])
 
         pl.when(y == 0)(early_image)
+        pl.when(y == 0)(opposite)
         arrived = xgot2.at[pl.ds(0, team - 1)]
         remote(arrived, arrived, *xgather, **member(lax.rem(seat + 1, team))).wait()
         finish = exchange(

time: 76.2 us -> 75.7 us (level)
  no operation moved by 1% of the time
where the time goes in v2:
time: 75.7 us; the launch traced here: 75.6 us
  Pallas kernels  72.9 us (96%)
  local copies, waits for them, and re-layouts  2.02 us (3%)
    pallas_call x1, Pallas kernels, shards(): pl.pallas_call(functools.partial(whole_kernel, nr, nc), out_shape=(pltpu....  72.9 us
    unnamed x2, local copies, waits for them, and re-layouts  2.02 us

profile of v2, /device:TPU:0, one launch (start us, length us, event | category | flops | bytes accessed | tf_op | source)
XLA Modules:
  0.0 75.6 jit_solution(5821746103918650782)
XLA Ops:
  0.6 72.9 %krylov.1 = (bf16[8192,128]{1,0:T(8,128)(2,1)S(1)}, f32[512,128]{1,0:T(8,128)S(1)}) custom-call(bf16[8192,128]{1,0:T(8,128)(2,1)} %basis.1, bf16[32,256,256]{2,1,0:T(8,128)(2,1)} %lower.1, bf16[32,256,256]{2,1,0:T(8,128)(2,1)} %diag.1, bf16[32,256,256]{2,1,0:T(8,128)(2,1)} %upper.1, bf16[32,256,256]{2,1,0:T(8,128)(2,1)} %inverse.1), custom_call_target="tpu_custom_call" | custom-call | flops 7516192768 | bytes 16777216 | tf_op jit(solution)/shard_map/krylov/pallas_call | solution.py:780
  73.5 1.3 %copy.9 = bf16[8192,128]{1,0:T(8,128)(2,1)} copy(bf16[8192,128]{1,0:T(8,128)(2,1)S(1)} %get-tuple-element.2) | data formatting | bytes 4194304
  74.9 0.7 copy.10
